TPU v7x, 32 devices: a whole 2x2x4 slice. The times are simulated.
32 devices in a mesh: dp: 4 (over z), expert: 8 (over y, x, core).
Axes of the slice: x: 2, y: 2, z: 4, core: 2. Of those that a mesh axis runs over, the one named last changes fastest.
Arguments:
- tokens: bfloat16 [256, 192, 1024], P(None, ('dp', 'expert')), may hold values from -200 to 200
- grad_out: bfloat16 [256, 192, 1024], P(None, ('dp', 'expert')), may hold values from -6 to 6
- slot_out: bfloat16 [512, 192, 1024], P('expert', 'dp'), may hold values from -6 to 6
- slot_params: bfloat16 [512, 1024], P('expert'), may hold values from -2 to 2
Outputs:
- grad_tokens: bfloat16 [256, 192, 1024], P(None, ('dp', 'expert'))
- grad_slot_out: bfloat16 [512, 192, 1024], P('expert', 'dp')
- grad_params: float32 [512, 1024], P('expert', 'dp')
All inputs are finite; a program needn't handle non-finite values.
Results may differ from a plain program's by a relative error of at most 0.018.
Values may be sent and summed in bfloat16 or wider, within the bound.
A program may use at most 128 MiB of HBM per device.

v0:
```python
import jax
import jax.numpy as jnp
from jax import lax
from jax.sharding import PartitionSpec as P


def fetch_outputs(slot_out, owners):
    own_slots, img_all, width = slot_out.shape
    shaped = slot_out.reshape(own_slots, owners, img_all // owners, width)
    arrived = lax.all_to_all(shaped, "expert", split_axis=1, concat_axis=0, tiled=True)
    return arrived.reshape(own_slots * owners, img_all // owners, width)


def return_grads(grad_slot, owners):
    all_slots, img_rows, width = grad_slot.shape
    shaped = grad_slot.reshape(owners, all_slots // owners, img_rows, width)
    arrived = lax.all_to_all(shaped, "expert", split_axis=0, concat_axis=2, tiled=True)
    return arrived.reshape(all_slots // owners, owners * img_rows, width)


def logit_grads(grad_comb, combine):
    rowdot = jnp.sum(combine * grad_comb, axis=-1, keepdims=True)
    return (combine * (grad_comb - rowdot)).astype(jnp.bfloat16)


def per_device(tokens, grad_out, slot_out, slot_params):
    owners = lax.axis_size("expert")
    all_params = lax.all_gather(slot_params, "expert", axis=0, tiled=True)
    logits = jnp.einsum("tbd,sd->tbs", tokens, all_params, preferred_element_type=jnp.float32)
    combine = jax.nn.softmax(logits, axis=-1)
    combine_low = combine.astype(jnp.bfloat16)
    slot_rows = fetch_outputs(slot_out, owners)
    grad_slot = jnp.einsum(
        "tbs,tbd->sbd", combine_low, grad_out, preferred_element_type=jnp.float32
    ).astype(jnp.bfloat16)
    grad_slot_out = return_grads(grad_slot, owners)
    grad_comb = jnp.einsum("tbd,sbd->tbs", grad_out, slot_rows, preferred_element_type=jnp.float32)
    grad_logits = logit_grads(grad_comb, combine)
    grad_tok = jnp.einsum(
        "tbs,sd->tbd", grad_logits, all_params, preferred_element_type=jnp.float32
    ).astype(jnp.bfloat16)
    param_part = jnp.einsum("tbs,tbd->sd", grad_logits, tokens, preferred_element_type=jnp.float32)
    owned = lax.psum_scatter(
        param_part.astype(jnp.bfloat16), "expert", scatter_dimension=0, tiled=True
    )
    grad_params = lax.psum_scatter(owned, "dp", scatter_dimension=1, tiled=True).astype(jnp.float32)
    return (grad_tok, grad_slot_out, grad_params)


def solution(mesh):
    return jax.shard_map(
        per_device,
        mesh=mesh,
        in_specs=(
            P(None, ("dp", "expert"), None),
            P(None, ("dp", "expert"), None),
            P("expert", "dp", None),
            P("expert", None),
        ),
        out_specs=(P(None, ("dp", "expert"), None), P("expert", "dp", None), P("expert", "dp")),
        check_vma=False,
    )
```

profile of v0, /device:TPU:0, one launch (start us, length us, event | category | flops | bytes accessed | tf_op | source)
XLA Modules:
  0.0 202.6 jit_solution(12654161094282766128)
XLA Ops:
  7.2 0.0 copy-start
  7.2 9.1 %copy.12 = bf16[64,48,1024]{2,0,1:T(8,128)(2,1)} copy(bf16[64,48,1024]{2,1,0:T(8,128)(2,1)} %param.6) | data formatting | bytes 12582912 | tf_op args[2]
  16.3 5.2 %all-to-all-start = ((bf16[64,8,6,1024]{3,0,2,1:T(8,128)(2,1)}), bf16[64,8,6,1024]{3,0,2,1:T(8,128)(2,1)}, u32[]{:S(2)}, u32[]{:S(2)}) async-start(bf16[64,8,6,1024]{3,0,2,1:T(8,128)(2,1)} %bitcast.38), calls=%async_computation | async-start | bytes 12582912 | tf_op jit(solution)/shard_map/all_to_all | solution.py:10
  21.5 0.0 all-gather.2.cloned.1.call-start
  21.6 0.7 all-gather.2.cloned.1.call-update
  22.3 45.9 %all-gather.2.cloned.1.call-done = bf16[512,1024]{1,0:T(8,128)(2,1)} async-done(((bf16[64,1024]{1,0:T(8,128)(2,1)}), bf16[512,1024]{1,0:T(8,128)(2,1)}) %all-gather.2.cloned.1.call-update) | async-done | bytes 1048592 | tf_op jit(solution)/shard_map/all_gather | solution.py:28
  68.2 4.1 %fusion.6 = f32[256,6,512]{2,0,1:T(8,128)S(1)} fusion(bf16[256,6,1024]{2,0,1:T(8,128)(2,1)} %param.4, bf16[512,1024]{1,0:T(8,128)(2,1)} %all-gather.2.cloned.1.call-done), kind=kOutput, calls=%fused_computation.13 | convolution fusion | flops 1610612736 | bytes 7340032 | tf_op jit(solution)/shard_map/tbd,sd->tbs/dot_general | solution.py:29
  72.3 2.5 %fusion.8 = (f32[256,6]{0,1:T(8,128)S(1)}, f32[256,6,512]{2,0,1:T(8,128)}) fusion(f32[256,6,512]{2,0,1:T(8,128)S(1)} %fusion.6), kind=kOutput, calls=%fused_computation.15 | output fusion | flops 1573375 | bytes 6297600 | tf_op jit(solution)/shard_map/sub | solution.py:30
  74.8 0.1 copy-done.2
  74.9 11.4 %convolution_convert_fusion = bf16[6,512,1024]{2,1,0:T(8,128)(2,1)} fusion(bf16[256,6,1024]{2,0,1:T(8,128)(2,1)S(1)} %copy-done, f32[256,6]{0,1:T(8,128)S(1)} %get-tuple-element.6, f32[256,6,512]{2,0,1:T(8,128)} %copy-done.2), kind=kOutput, calls=%fused_computation.1 | convolution fusion | flops 1616119808 | bytes 12589056 | tf_op jit(solution)/shard_map/tbs,tbd->sbd/dot_general | solution.py:33
  86.3 6.7 %copy.16 = bf16[8,64,6,1024]{3,1,2,0:T(8,128)(2,1)} copy(bf16[8,64,6,1024]{3,1,0,2:T(8,128)(2,1)} %bitcast.40) | data formatting | bytes 12582912 | tf_op jit(solution)/shard_map/reshape | solution.py:16
  93.0 4.6 %all-to-all-done = bf16[64,8,6,1024]{3,0,2,1:T(8,128)(2,1)} async-done(((bf16[64,8,6,1024]{3,0,2,1:T(8,128)(2,1)}), bf16[64,8,6,1024]{3,0,2,1:T(8,128)(2,1)}, u32[]{:S(2)}, u32[]{:S(2)}) %all-to-all-start) | async-done | bytes 6291488 | tf_op jit(solution)/shard_map/all_to_all | solution.py:10
  97.6 4.8 %all-to-all-start.1 = ((bf16[8,64,6,1024]{3,1,2,0:T(8,128)(2,1)}), bf16[8,64,6,1024]{3,1,2,0:T(8,128)(2,1)}, u32[]{:S(2)}, u32[]{:S(2)}) async-start(bf16[8,64,6,1024]{3,1,2,0:T(8,128)(2,1)} %copy.16), calls=%async_computation.1 | async-start | bytes 12582912 | tf_op jit(solution)/shard_map/all_to_all | solution.py:17
  102.4 0.2 reduce-scatter.3.cloned.1.call-start
  102.6 0.0 copy-start.1
  102.7 3.7 %copy.13 = bf16[8,64,1,6,1024]{4,1,0,3,2:T(8,128)(2,1)S(1)} copy(bf16[8,64,1,6,1024]{4,1,3,0,2:T(8,128)(2,1)} %bitcast.3) | data formatting | bytes 12582912 | tf_op jit(solution)/shard_map/all_to_all | solution.py:10
  106.3 0.0 copy-done.1
  106.4 2.0 fusion.1
  108.3 0.0 copy-start.4
  108.3 0.6 fusion.3
  109.0 0.0 copy-start.3
  109.0 1.1 copy-done.3
  110.1 0.7 copy-done.4
  110.8 2.8 %bitcast_convert_fusion = bf16[512,1024]{1,0:T(8,128)(2,1)} fusion(bf16[256,6,512]{2,0,1:T(8,128)(2,1)S(1)} %fusion.3, bf16[256,6,1024]{2,0,1:T(8,128)(2,1)S(1)} %copy-done.4), kind=kOutput, calls=%fused_computation.9 | convolution fusion | flops 1611137024 | bytes 5767168 | tf_op jit(solution)/shard_map/tbs,tbd->sd/dot_general | solution.py:42
  113.6 0.0 reduce-scatter.3.cloned.1.call-update
  113.6 0.0 reduce-scatter.5.cloned.1.call-start
  113.7 60.1 %reduce-scatter.3.cloned.1.call-done = bf16[64,1024]{1,0:T(8,128)(2,1)} async-done(((bf16[512,1024]{1,0:T(8,128)(2,1)}), bf16[64,1024]{1,0:T(8,128)(2,1)}) %reduce-scatter.3.cloned.1.call-update) | async-done | bytes 131088 | tf_op jit(solution)/shard_map/reduce_scatter | solution.py:43
  173.8 0.0 reduce-scatter.5.cloned.1.call-update
  173.8 5.2 %convolution_convert_fusion.1 = bf16[256,6,1024]{2,0,1:T(8,128)(2,1)} fusion(bf16[256,6,512]{2,0,1:T(8,128)(2,1)} %copy-done.3, bf16[512,1024]{1,0:T(8,128)(2,1)} %all-gather.2.cloned.1.call-done), kind=kOutput, calls=%fused_computation.8 | convolution fusion | flops 1612185600 | bytes 5767168 | tf_op jit(solution)/shard_map/tbs,sd->tbd/dot_general | solution.py:39
  179.0 9.0 %copy.18 = bf16[64,48,1024]{2,1,0:T(8,128)(2,1)} copy(bf16[64,48,1024]{2,0,1:T(8,128)(2,1)} %bitcast.10) | data formatting | bytes 12582912
  188.0 6.6 %reduce-scatter.5.cloned.1.call-done = bf16[64,256]{1,0:T(8,128)(2,1)} async-done(((bf16[64,1024]{1,0:T(8,128)(2,1)}), bf16[64,256]{1,0:T(8,128)(2,1)}) %reduce-scatter.5.cloned.1.call-update) | async-done | bytes 32784 | tf_op jit(solution)/shard_map/reduce_scatter | solution.py:46
  194.6 1.4 convert_element_type.27
  (3 shorter events, 0.0 us)
Async XLA Ops:
  7.2 67.7 %copy-start = (bf16[256,6,1024]{2,0,1:T(8,128)(2,1)S(1)}, bf16[256,6,1024]{2,0,1:T(8,128)(2,1)}, u32[]{:S(2)}) copy-start(bf16[256,6,1024]{2,0,1:T(8,128)(2,1)} %param.5) | copy-start | bytes 9437188
  16.3 81.3 %all-to-all-start = ((bf16[64,8,6,1024]{3,0,2,1:T(8,128)(2,1)}), bf16[64,8,6,1024]{3,0,2,1:T(8,128)(2,1)}, u32[]{:S(2)}, u32[]{:S(2)}) async-start(bf16[64,8,6,1024]{3,0,2,1:T(8,128)(2,1)} %bitcast.38), calls=%async_computation | async-start | bytes 12582912 | tf_op jit(solution)/shard_map/all_to_all | solution.py:10
  21.5 46.6 %all-gather.2.cloned.1.call-start = ((), (), s32[]{:S(2)}) async-start(), calls=%async_computation.4 | async-start | bytes 1179648 | tf_op jit(solution)/shard_map/all_gather | solution.py:28
  72.3 2.7 %copy-start.2 = (f32[256,6,512]{2,0,1:T(8,128)}, f32[256,6,512]{2,0,1:T(8,128)S(1)}, u32[]{:S(2)}) copy-start(f32[256,6,512]{2,0,1:T(8,128)S(1)} %fusion.6) | copy-start | bytes 9437188
  97.6 81.4 %all-to-all-start.1 = ((bf16[8,64,6,1024]{3,1,2,0:T(8,128)(2,1)}), bf16[8,64,6,1024]{3,1,2,0:T(8,128)(2,1)}, u32[]{:S(2)}, u32[]{:S(2)}) async-start(bf16[8,64,6,1024]{3,1,2,0:T(8,128)(2,1)} %copy.16), calls=%async_computation.1 | async-start | bytes 12582912 | tf_op jit(solution)/shard_map/all_to_all | solution.py:17
  102.4 71.4 %reduce-scatter.3.cloned.1.call-start = ((), (), s32[]{:S(2)}) async-start(), calls=%async_computation.5 | async-start | bytes 1179648 | tf_op jit(solution)/shard_map/reduce_scatter | solution.py:43
  102.6 3.7 %copy-start.1 = (f32[256,6,512]{2,0,1:T(8,128)S(1)}, f32[256,6,512]{2,0,1:T(8,128)}, u32[]{:S(2)}) copy-start(f32[256,6,512]{2,0,1:T(8,128)} %get-tuple-element.7) | copy-start | bytes 9437188
  108.3 2.5 %copy-start.4 = (bf16[256,6,1024]{2,0,1:T(8,128)(2,1)S(1)}, bf16[256,6,1024]{2,0,1:T(8,128)(2,1)}, u32[]{:S(2)}) copy-start(bf16[256,6,1024]{2,0,1:T(8,128)(2,1)} %param.4) | copy-start | bytes 9437188
  109.0 1.1 copy-start.3
  113.6 81.0 %reduce-scatter.5.cloned.1.call-start = ((), (), s32[]{:S(2)}) async-start(), calls=%async_computation.6 | async-start | bytes 163840 | tf_op jit(solution)/shard_map/reduce_scatter | solution.py:46
Sparse Core Ops, SparseCore 0:
  24.2 43.8 all-gather.1
  113.7 60.0 reduce-scatter.2
  176.0 18.5 reduce-scatter.4
where the time goes:
time: 203 us
  waiting for transfers between devices  118 us (58%)
  local copies, waits for them, and re-layouts  30.5 us (15%)
  matrix products  25.4 us (13%)
  between operations  13.8 us (7%)
  starting transfers between devices  10.3 us (5%)
  other arithmetic  4.54 us (2%)
    reduce_scatter x1, waiting for transfers between devices, per_device(): lax.psum_scatter(param_part.astype(jnp.bfloat16), 'expert', scatter_dimen...  60.1 us
    all_gather x1, waiting for transfers between devices, per_device(): all_params = lax.all_gather(slot_params, 'expert', axis=0, tiled=True)  45.9 us
    unnamed x12, local copies, waits for them, and re-layouts  20.2 us
    dot_general x1, matrix products, per_device(): jnp.einsum('tbs,tbd->sbd', combine_low, grad_out, preferred_element_type=...  11.4 us
    reshape x1, local copies, waits for them, and re-layouts, return_grads(): shaped = grad_slot.reshape(owners, all_slots // owners, img_rows, width)  6.69 us
    reduce_scatter x1, waiting for transfers between devices, per_device(): lax.psum_scatter(owned, 'dp', scatter_dimension=1, tiled=True)  6.62 us
    all_to_all x1, starting transfers between devices, fetch_outputs(): lax.all_to_all(shaped, 'expert', split_axis=1, concat_axis=0, tiled=True)  5.2 us
    dot_general x1, matrix products, per_device(): jnp.einsum('tbs,sd->tbd', grad_logits, all_params, preferred_element_type...  5.17 us
  transfers between devices with their start and end apart: 5, of which 4 were waited for; matrix products, arithmetic and copies ran while one was open for 24% of the time, Pallas kernels for 0%

commit v1 on v0

--- a/solution.py
+++ b/solution.py
@@ -24,8 +24,21 @@
 
 
 def per_device(tokens, grad_out, slot_out, slot_params):
+
+    def manage_the_row(message):
+        amount_of = lax.axis_size("expert")
+        trail = list(map(lambda w: (w, (w + 1) % amount_of), range(amount_of)))
+
+        def windows_play(u_next):
+            if len(u_next) == amount_of:
+                return u_next
+            return windows_play([lax.ppermute(u_next[0], "expert", trail), *u_next])
+
+        t1 = jnp.concatenate(windows_play([message]), axis=0)
+        return jnp.roll(t1, (lax.axis_index("expert") + 1) * message.shape[0], axis=0)
+
     owners = lax.axis_size("expert")
-    all_params = lax.all_gather(slot_params, "expert", axis=0, tiled=True)
+    all_params = manage_the_row(slot_params)
     logits = jnp.einsum("tbd,sd->tbs", tokens, all_params, preferred_element_type=jnp.float32)
     combine = jax.nn.softmax(logits, axis=-1)
     combine_low = combine.astype(jnp.bfloat16)

time: 203 us -> 260 us (1.28)
  waiting for transfers between devices: 118 us -> 172 us
  local copies, waits for them, and re-layouts: 30.5 us -> 38.8 us
  matrix products: 25.4 us -> 19.1 us
    ppermute x0 -> x7, waiting for transfers between devices: none -> 105 us  [windows_play(): return windows_play([lax.ppermute(u_next[0], 'expert', trail), *u_next])]
    all_gather x1 -> x0, waiting for transfers between devices: 45.9 us -> none  [per_device(): all_params = lax.all_gather(slot_params, 'expert', axis=0, tiled=True)]
    unnamed x12 -> x45, local copies, waits for them, and re-layouts: 20.2 us -> 28.4 us
    all_to_all x1, waiting for transfers between devices: 4.6 us -> 0.01 us  [fetch_outputs(): lax.all_to_all(shaped, 'expert', split_axis=1, concat_axis=0, tiled=True)]
    dot_general x1, matrix products: 11.4 us -> 7.33 us  [per_device(): jnp.einsum('tbs,tbd->sbd', combine_low, grad_out, preferred_element_type=...]
  transfers between devices with their start and end apart: 5 -> 11, of which waited for: 4 -> 9; matrix products, arithmetic and copies ran while one was open for 24% -> 19% of each run, Pallas kernels for 0% -> 0%
where the time goes in v1:
time: 260 us; the launch traced here: 259 us
  waiting for transfers between devices  172 us (66%)
  local copies, waits for them, and re-layouts  38.8 us (15%)
  matrix products  19.1 us (7%)
  between operations  14.3 us (6%)
  starting transfers between devices  10.9 us (4%)
  other arithmetic  4.78 us (2%)
    ppermute x7, waiting for transfers between devices, windows_play(): return windows_play([lax.ppermute(u_next[0], 'expert', trail), *u_next])  105 us
    reduce_scatter x1, waiting for transfers between devices, per_device(): lax.psum_scatter(param_part.astype(jnp.bfloat16), 'expert', scatter_dimen...  60.2 us
    unnamed x45, local copies, waits for them, and re-layouts  28.4 us
    dot_general x1, matrix products, per_device(): jnp.einsum('tbs,tbd->sbd', combine_low, grad_out, preferred_element_type=...  7.33 us
    reshape x1, local copies, waits for them, and re-layouts, return_grads(): shaped = grad_slot.reshape(owners, all_slots // owners, img_rows, width)  6.68 us
    reduce_scatter x1, waiting for transfers between devices, per_device(): lax.psum_scatter(owned, 'dp', scatter_dimension=1, tiled=True)  6.55 us
    all_to_all x1, starting transfers between devices, fetch_outputs(): lax.all_to_all(shaped, 'expert', split_axis=1, concat_axis=0, tiled=True)  5.33 us
    dot_general x1, matrix products, per_device(): jnp.einsum('tbs,sd->tbd', grad_logits, all_params, preferred_element_type...  5.2 us
  transfers between devices with their start and end apart: 11, of which 9 were waited for; matrix products, arithmetic and copies ran while one was open for 19% of the time, Pallas kernels for 0%

profile of v1, /device:TPU:0, one launch (start us, length us, event | category | flops | bytes accessed | tf_op | source)
XLA Modules:
  0.0 259.4 jit_solution(9543488815251218017)
XLA Ops:
  7.2 9.1 %copy.10 = bf16[64,48,1024]{2,0,1:T(8,128)(2,1)} copy(bf16[64,48,1024]{2,1,0:T(8,128)(2,1)} %param.6) | data formatting | bytes 12582912 | tf_op args[2]
  16.3 5.3 %all-to-all-start = ((bf16[64,8,6,1024]{3,0,2,1:T(8,128)(2,1)}), bf16[64,8,6,1024]{3,0,2,1:T(8,128)(2,1)}, u32[]{:S(2)}, u32[]{:S(2)}) async-start(bf16[64,8,6,1024]{3,0,2,1:T(8,128)(2,1)} %bitcast.55), calls=%async_computation | async-start | bytes 12582912 | tf_op jit(solution)/shard_map/all_to_all | solution.py:10
  22.2 72.6 %collective-permute-done = bf16[64,1024]{1,0:T(8,128)(2,1)S(1)} collective-permute-done((bf16[64,1024]{1,0:T(8,128)(2,1)S(1)}, bf16[64,1024]{1,0:T(8,128)(2,1)S(1)}, u32[]{:S(2)}, u32[]{:S(2)}) %collective-permute-start) | collective-permute-done | bytes 131104 | tf_op jit(solution)/shard_map/ppermute | solution.py:35
  94.8 5.3 %collective-permute-done.1 = bf16[64,1024]{1,0:T(8,128)(2,1)S(1)} collective-permute-done((bf16[64,1024]{1,0:T(8,128)(2,1)S(1)}, bf16[64,1024]{1,0:T(8,128)(2,1)S(1)}, u32[]{:S(2)}, u32[]{:S(2)}) %collective-permute-start.1) | collective-permute-done | bytes 131104 | tf_op jit(solution)/shard_map/ppermute | solution.py:35
  100.1 5.3 %collective-permute-done.2 = bf16[64,1024]{1,0:T(8,128)(2,1)S(1)} collective-permute-done((bf16[64,1024]{1,0:T(8,128)(2,1)S(1)}, bf16[64,1024]{1,0:T(8,128)(2,1)S(1)}, u32[]{:S(2)}, u32[]{:S(2)}) %collective-permute-start.2) | collective-permute-done | bytes 131104 | tf_op jit(solution)/shard_map/ppermute | solution.py:35
  106.0 5.3 %collective-permute-done.3 = bf16[64,1024]{1,0:T(8,128)(2,1)S(1)} collective-permute-done((bf16[64,1024]{1,0:T(8,128)(2,1)S(1)}, bf16[64,1024]{1,0:T(8,128)(2,1)S(1)}, u32[]{:S(2)}, u32[]{:S(2)}) %collective-permute-start.3) | collective-permute-done | bytes 131104 | tf_op jit(solution)/shard_map/ppermute | solution.py:35
  112.0 5.3 %collective-permute-done.4 = bf16[64,1024]{1,0:T(8,128)(2,1)S(1)} collective-permute-done((bf16[64,1024]{1,0:T(8,128)(2,1)S(1)}, bf16[64,1024]{1,0:T(8,128)(2,1)S(1)}, u32[]{:S(2)}, u32[]{:S(2)}) %collective-permute-start.4) | collective-permute-done | bytes 131104 | tf_op jit(solution)/shard_map/ppermute | solution.py:35
  117.3 0.7 copy-done.9
  117.9 5.4 %collective-permute-done.5 = bf16[64,1024]{1,0:T(8,128)(2,1)} collective-permute-done((bf16[64,1024]{1,0:T(8,128)(2,1)S(1)}, bf16[64,1024]{1,0:T(8,128)(2,1)}, u32[]{:S(2)}, u32[]{:S(2)}) %collective-permute-start.5) | collective-permute-done | bytes 131104 | tf_op jit(solution)/shard_map/ppermute | solution.py:35
  123.3 5.6 %collective-permute-done.6 = bf16[64,1024]{1,0:T(8,128)(2,1)} collective-permute-done((bf16[64,1024]{1,0:T(8,128)(2,1)}, bf16[64,1024]{1,0:T(8,128)(2,1)}, u32[]{:S(2)}, u32[]{:S(2)}) %collective-permute-start.6) | collective-permute-done | bytes 131104 | tf_op jit(solution)/shard_map/ppermute | solution.py:35
  128.9 0.9 constant_dynamic-update-slice_fusion.15
  129.8 0.9 constant_dynamic-update-slice_fusion.14
  130.8 0.9 constant_dynamic-update-slice_fusion.13
  131.7 0.9 constant_dynamic-update-slice_fusion.12
  132.6 0.9 constant_dynamic-update-slice_fusion.11
  133.6 0.9 constant_dynamic-update-slice_fusion.7
  134.5 0.9 constant_dynamic-update-slice_fusion.6
  135.6 1.8 fusion.10
  137.4 2.7 %fusion.20 = (f32[256,6]{0,1:T(8,128)S(1)}, f32[256,6,512]{0,2,1:T(8,128)}) fusion(f32[512,256,6]{1,0,2:T(8,128)S(1)} %fusion.10), kind=kOutput, calls=%fused_computation.38 | output fusion | flops 1573375 | bytes 6297600 | tf_op jit(solution)/shard_map/sub | solution.py:43
  140.1 7.3 %convolution_convert_fusion = bf16[6,512,1024]{2,1,0:T(8,128)(2,1)} fusion(bf16[256,6,1024]{2,0,1:T(8,128)(2,1)S(1)} %copy-done, f32[256,6]{0,1:T(8,128)S(1)} %get-tuple-element.6, f32[512,256,6]{1,0,2:T(8,128)} %copy-done.2), kind=kOutput, calls=%fused_computation.1 | convolution fusion | flops 1616119808 | bytes 12589056 | tf_op jit(solution)/shard_map/tbs,tbd->sbd/dot_general | solution.py:46
  147.5 6.7 %copy.13 = bf16[8,64,6,1024]{3,1,2,0:T(8,128)(2,1)} copy(bf16[8,64,6,1024]{3,1,0,2:T(8,128)(2,1)} %bitcast.57) | data formatting | bytes 12582912 | tf_op jit(solution)/shard_map/reshape | solution.py:16
  154.1 4.8 %all-to-all-start.1 = ((bf16[8,64,6,1024]{3,1,2,0:T(8,128)(2,1)}), bf16[8,64,6,1024]{3,1,2,0:T(8,128)(2,1)}, u32[]{:S(2)}, u32[]{:S(2)}) async-start(bf16[8,64,6,1024]{3,1,2,0:T(8,128)(2,1)} %copy.13), calls=%async_computation.1 | async-start | bytes 12582912 | tf_op jit(solution)/shard_map/all_to_all | solution.py:17
  159.2 3.7 %copy.11 = bf16[8,64,1,6,1024]{4,1,0,3,2:T(8,128)(2,1)S(1)} copy(bf16[8,64,1,6,1024]{4,1,3,0,2:T(8,128)(2,1)} %bitcast.4) | data formatting | bytes 12582912 | tf_op jit(solution)/shard_map/all_to_all | solution.py:10
  162.9 1.9 fusion.1
  164.8 0.7 fusion.3
  165.6 1.1 copy-done.3
  167.3 2.8 %bitcast_convert_fusion = bf16[512,1024]{1,0:T(8,128)(2,1)} fusion(bf16[256,6,512]{0,2,1:T(8,128)(2,1)S(1)} %fusion.3, bf16[256,6,1024]{2,0,1:T(8,128)(2,1)S(1)} %copy-done.13), kind=kOutput, calls=%fused_computation.12 | convolution fusion | flops 1611137024 | bytes 5767168 | tf_op jit(solution)/shard_map/tbs,tbd->sd/dot_general | solution.py:55
  170.1 60.2 %reduce-scatter.3.cloned.1.call-done = bf16[64,1024]{1,0:T(8,128)(2,1)} async-done(((bf16[512,1024]{1,0:T(8,128)(2,1)}), bf16[64,1024]{1,0:T(8,128)(2,1)}) %reduce-scatter.3.cloned.1.call-update) | async-done | bytes 131088 | tf_op jit(solution)/shard_map/reduce_scatter | solution.py:56
  230.4 5.2 %convolution_convert_fusion.1 = bf16[256,6,1024]{2,0,1:T(8,128)(2,1)} fusion(bf16[256,6,512]{0,2,1:T(8,128)(2,1)} %copy-done.3, bf16[1024,1024]{1,0:T(8,128)(2,1)} %copy-done.11, s32[]{:T(128)S(6)} %select_n.14), kind=kOutput, calls=%fused_computation.11 | convolution fusion | flops 1612185600 | bytes 5767172 | tf_op jit(solution)/shard_map/tbs,sd->tbd/dot_general | solution.py:52
  235.6 9.0 %copy.14 = bf16[64,48,1024]{2,1,0:T(8,128)(2,1)} copy(bf16[64,48,1024]{2,0,1:T(8,128)(2,1)} %bitcast.11) | data formatting | bytes 12582912
  244.6 6.5 %reduce-scatter.5.cloned.1.call-done = bf16[64,256]{1,0:T(8,128)(2,1)} async-done(((bf16[64,1024]{1,0:T(8,128)(2,1)}), bf16[64,256]{1,0:T(8,128)(2,1)}) %reduce-scatter.5.cloned.1.call-update) | async-done | bytes 32784 | tf_op jit(solution)/shard_map/reduce_scatter | solution.py:59
  251.1 1.4 convert_element_type.27
  (48 shorter events, 2.9 us)
Async XLA Ops:
  7.2 133.0 %copy-start = (bf16[256,6,1024]{2,0,1:T(8,128)(2,1)S(1)}, bf16[256,6,1024]{2,0,1:T(8,128)(2,1)}, u32[]{:S(2)}) copy-start(bf16[256,6,1024]{2,0,1:T(8,128)(2,1)} %param.5) | copy-start | bytes 9437188
  16.3 5.3 %copy-start.4 = (bf16[64,1024]{1,0:T(8,128)(2,1)S(1)}, bf16[64,1024]{1,0:T(8,128)(2,1)}, u32[]{:S(2)}) copy-start(bf16[64,1024]{1,0:T(8,128)(2,1)} %param.7) | copy-start | bytes 393220
  16.3 137.8 %all-to-all-start = ((bf16[64,8,6,1024]{3,0,2,1:T(8,128)(2,1)}), bf16[64,8,6,1024]{3,0,2,1:T(8,128)(2,1)}, u32[]{:S(2)}, u32[]{:S(2)}) async-start(bf16[64,8,6,1024]{3,0,2,1:T(8,128)(2,1)} %bitcast.55), calls=%async_computation | async-start | bytes 12582912 | tf_op jit(solution)/shard_map/all_to_all | solution.py:10
  21.7 73.1 %collective-permute-start = (bf16[64,1024]{1,0:T(8,128)(2,1)S(1)}, bf16[64,1024]{1,0:T(8,128)(2,1)S(1)}, u32[]{:S(2)}, u32[]{:S(2)}) collective-permute-start(bf16[64,1024]{1,0:T(8,128)(2,1)S(1)} %copy-done.4), channel_id=1, source_target_pairs={{0,1},{1,2},{2,3},{3,4},{4,5},{5,6},{6,7},{7,0},{8,9},{9,10},{10,1... | collective-permute-start | bytes 393224 | tf_op jit(solution)/shard_map/ppermute | solution.py:35
  94.8 5.3 %collective-permute-start.1 = (bf16[64,1024]{1,0:T(8,128)(2,1)S(1)}, bf16[64,1024]{1,0:T(8,128)(2,1)S(1)}, u32[]{:S(2)}, u32[]{:S(2)}) collective-permute-start(bf16[64,1024]{1,0:T(8,128)(2,1)S(1)} %collective-permute-done), channel_id=1, source_target_pairs={{0,1},{1,2},{2,3},{3,4},{4,5},{5,6},{6,7},{7,0},{8,9},{9,10},{10,1... | collective-permute-start | bytes 393224 | tf_op jit(solution)/shard_map/ppermute | solution.py:35
  100.1 5.3 %collective-permute-start.2 = (bf16[64,1024]{1,0:T(8,128)(2,1)S(1)}, bf16[64,1024]{1,0:T(8,128)(2,1)S(1)}, u32[]{:S(2)}, u32[]{:S(2)}) collective-permute-start(bf16[64,1024]{1,0:T(8,128)(2,1)S(1)} %collective-permute-done.1), channel_id=1, source_target_pairs={{0,1},{1,2},{2,3},{3,4},{4,5},{5,6},{6,7},{7,0},{8,9},{9,10},{10,1... | collective-permute-start | bytes 393224 | tf_op jit(solution)/shard_map/ppermute | solution.py:35
  105.4 0.7 copy-start.5
  106.0 5.3 %collective-permute-start.3 = (bf16[64,1024]{1,0:T(8,128)(2,1)S(1)}, bf16[64,1024]{1,0:T(8,128)(2,1)S(1)}, u32[]{:S(2)}, u32[]{:S(2)}) collective-permute-start(bf16[64,1024]{1,0:T(8,128)(2,1)S(1)} %collective-permute-done.2), channel_id=1, source_target_pairs={{0,1},{1,2},{2,3},{3,4},{4,5},{5,6},{6,7},{7,0},{8,9},{9,10},{10,1... | collective-permute-start | bytes 393224 | tf_op jit(solution)/shard_map/ppermute | solution.py:35
  111.3 0.7 copy-start.7
  112.0 5.3 %collective-permute-start.4 = (bf16[64,1024]{1,0:T(8,128)(2,1)S(1)}, bf16[64,1024]{1,0:T(8,128)(2,1)S(1)}, u32[]{:S(2)}, u32[]{:S(2)}) collective-permute-start(bf16[64,1024]{1,0:T(8,128)(2,1)S(1)} %collective-permute-done.3), channel_id=1, source_target_pairs={{0,1},{1,2},{2,3},{3,4},{4,5},{5,6},{6,7},{7,0},{8,9},{9,10},{10,1... | collective-permute-start | bytes 393224 | tf_op jit(solution)/shard_map/ppermute | solution.py:35
  117.3 0.7 copy-start.9
  117.9 5.4 %collective-permute-start.5 = (bf16[64,1024]{1,0:T(8,128)(2,1)S(1)}, bf16[64,1024]{1,0:T(8,128)(2,1)}, u32[]{:S(2)}, u32[]{:S(2)}) collective-permute-start(bf16[64,1024]{1,0:T(8,128)(2,1)S(1)} %collective-permute-done.4), channel_id=1, source_target_pairs={{0,1},{1,2},{2,3},{3,4},{4,5},{5,6},{6,7},{7,0},{8,9},{9,10},{10,1... | collective-permute-start | bytes 393224 | tf_op jit(solution)/shard_map/ppermute | solution.py:35
  123.3 5.6 %collective-permute-start.6 = (bf16[64,1024]{1,0:T(8,128)(2,1)}, bf16[64,1024]{1,0:T(8,128)(2,1)}, u32[]{:S(2)}, u32[]{:S(2)}) collective-permute-start(bf16[64,1024]{1,0:T(8,128)(2,1)} %collective-permute-done.5), channel_id=1, source_target_pairs={{0,1},{1,2},{2,3},{3,4},{4,5},{5,6},{6,7},{7,0},{8,9},{9,10},{10,1... | collective-permute-start | bytes 393224 | tf_op jit(solution)/shard_map/ppermute | solution.py:35
  123.3 12.1 %copy-start.10 = (bf16[64,1024]{1,0:T(8,128)(2,1)S(1)}, bf16[64,1024]{1,0:T(8,128)(2,1)}, u32[]{:S(2)}) copy-start(bf16[64,1024]{1,0:T(8,128)(2,1)} %copy-done.9) | copy-start | bytes 393220
  123.3 12.1 %copy-start.8 = (bf16[64,1024]{1,0:T(8,128)(2,1)S(1)}, bf16[64,1024]{1,0:T(8,128)(2,1)}, u32[]{:S(2)}) copy-start(bf16[64,1024]{1,0:T(8,128)(2,1)} %copy-done.7) | copy-start | bytes 393220
  123.3 12.1 %copy-start.6 = (bf16[64,1024]{1,0:T(8,128)(2,1)S(1)}, bf16[64,1024]{1,0:T(8,128)(2,1)}, u32[]{:S(2)}) copy-start(bf16[64,1024]{1,0:T(8,128)(2,1)} %copy-done.5) | copy-start | bytes 393220
  123.3 12.2 %copy-start.12 = (bf16[256,6,1024]{2,0,1:T(8,128)(2,1)S(1)}, bf16[256,6,1024]{2,0,1:T(8,128)(2,1)}, u32[]{:S(2)}) copy-start(bf16[256,6,1024]{2,0,1:T(8,128)(2,1)} %param.4) | copy-start | bytes 9437188
  135.6 1.9 copy-start.11
  137.4 2.7 %copy-start.2 = (f32[512,256,6]{1,0,2:T(8,128)}, f32[512,256,6]{1,0,2:T(8,128)S(1)}, u32[]{:S(2)}) copy-start(f32[512,256,6]{1,0,2:T(8,128)S(1)} %fusion.10) | copy-start | bytes 9437188
  154.1 81.4 %all-to-all-start.1 = ((bf16[8,64,6,1024]{3,1,2,0:T(8,128)(2,1)}), bf16[8,64,6,1024]{3,1,2,0:T(8,128)(2,1)}, u32[]{:S(2)}, u32[]{:S(2)}) async-start(bf16[8,64,6,1024]{3,1,2,0:T(8,128)(2,1)} %copy.13), calls=%async_computation.1 | async-start | bytes 12582912 | tf_op jit(solution)/shard_map/all_to_all | solution.py:17
  159.0 71.4 %reduce-scatter.3.cloned.1.call-start = ((), (), s32[]{:S(2)}) async-start(), calls=%async_computation.4 | async-start | bytes 1179648 | tf_op jit(solution)/shard_map/reduce_scatter | solution.py:56
  159.2 3.7 %copy-start.1 = (f32[256,6,512]{0,2,1:T(8,128)S(1)}, f32[256,6,512]{0,2,1:T(8,128)}, u32[]{:S(2)}) copy-start(f32[256,6,512]{0,2,1:T(8,128)} %get-tuple-element.7) | copy-start | bytes 9437188
  164.8 2.4 copy-start.13
  165.5 1.1 copy-start.3
  170.1 81.1 %reduce-scatter.5.cloned.1.call-start = ((), (), s32[]{:S(2)}) async-start(), calls=%async_computation.5 | async-start | bytes 163840 | tf_op jit(solution)/shard_map/reduce_scatter | solution.py:59
Sparse Core Ops, SparseCore 0:
  170.2 60.0 reduce-scatter.2
  232.6 18.5 reduce-scatter.4
